TPU v7x, 32 devices: a whole 2x2x4 slice. The times are simulated.
32 devices in a mesh: dp: 4 (over z), expert: 2 (over x), tensor: 4 (over y, core).
Axes of the slice: x: 2, y: 2, z: 4, core: 2. Of those that a mesh axis runs over, the one named last changes fastest.
Arguments:
- tokens: bfloat16 [256, 4096], P(('dp', 'expert', 'tensor')), may hold values from -6 to 6
- out_grad: bfloat16 [256, 4096], P(('dp', 'expert', 'tensor')), may hold values from -4 to 4
- route_probs: float32 [256, 2], P(('dp', 'expert')), may hold values from 0.2 to 1
- expert_ids: int32 [256, 2], P(('dp', 'expert')), may hold values from 0 to 7, as said below
- slot_index: int32 [256, 2], P(('dp', 'expert')), may hold values from 0 to 10, as said below
- w_gate: bfloat16 [8, 4096, 7168], P('expert', 'dp', 'tensor'), may hold values from -0.09375 to 0.09375
- w_up: bfloat16 [8, 4096, 7168], P('expert', 'dp', 'tensor'), may hold values from -0.09375 to 0.09375
- w_down: bfloat16 [8, 7168, 4096], P('expert', 'tensor', 'dp'), may hold values from -0.0625 to 0.0625
Outputs:
- token_grad: bfloat16 [256, 4096], P(('dp', 'expert', 'tensor'))
- grad_gate: bfloat16 [8, 4096, 7168], P('expert', 'dp', 'tensor')
- grad_up: bfloat16 [8, 4096, 7168], P('expert', 'dp', 'tensor')
- grad_down: bfloat16 [8, 7168, 4096], P('expert', 'tensor', 'dp')
Inputs may be any that keep to these rules, and one draw needn't show every extreme that they name: `expert_ids`: the 2 entries of a token are different experts. slot_index[t, k] counts the earlier routes to expert_ids[t, k] within the token's routing block of 32 rows, in order of tokens and then of routes; the value 10 marks a route past the capacity, which is dropped (a count of 10 or more is given as 10). In every draw some expert is filled to 10 slots in every block.
All inputs are finite; a program needn't handle non-finite values.
Results may differ from a plain program's by a relative error of at most 0.011.
Values may be sent and summed in bfloat16 or wider, within the bound.
No kernel may reach another device: no remote copies, remote signals or barrier semaphores. Data moves between devices by JAX's collectives and lax.ppermute only.
A program may use at most 192 MiB of HBM per device.

v0:
```python
import jax
import jax.numpy as jnp
from jax import lax
from jax.sharding import PartitionSpec as P

EXPERTS = 8
TOP = 2


def route_tables(expert_ids, slot_index, capacity):
    target = slot_index * EXPERTS + expert_ids
    target = jnp.where(slot_index < capacity, target, -1)
    places = jnp.arange(capacity * EXPERTS, dtype=jnp.int32)
    return [(places[:, None] == target[None, :, k]).astype(jnp.bfloat16) for k in range(TOP)]


def swiglu_back(pre_gate, pre_up, grad_hidden):
    sigmoid_gate = jax.nn.sigmoid(pre_gate)
    silu_gate = pre_gate * sigmoid_gate
    hidden = (silu_gate * pre_up).astype(jnp.bfloat16)
    up_delta = (grad_hidden * silu_gate).astype(jnp.bfloat16)
    gate_delta = (
        grad_hidden * pre_up * sigmoid_gate * (1.0 + pre_gate * (1.0 - sigmoid_gate))
    ).astype(jnp.bfloat16)
    return (hidden, gate_delta, up_delta)


def shards(tokens, out_grad, route_probs, expert_ids, slot_index, w_gate, w_up, w_down):
    block_x, block_dy = (
        lax.all_gather(tokens, "tensor", axis=0, tiled=True),
        lax.all_gather(out_grad, "tensor", axis=0, tiled=True),
    )
    block_rows = block_x.shape[0]
    model_width = block_x.shape[1]
    capacity = 5 * block_rows * TOP // (4 * EXPERTS)
    tables = route_tables(expert_ids, slot_index, capacity)
    table_sum = tables[0] + tables[1]
    x_buf = jnp.dot(table_sum, block_x, preferred_element_type=jnp.float32).astype(jnp.bfloat16)
    grad_buf = jnp.zeros((capacity * EXPERTS, model_width), jnp.float32)
    for k in range(TOP):
        scaled = (route_probs[:, k : k + 1] * block_dy.astype(jnp.float32)).astype(jnp.bfloat16)
        grad_buf = grad_buf + jnp.dot(tables[k], scaled, preferred_element_type=jnp.float32)
    grad_buf = grad_buf.astype(jnp.bfloat16)
    recv_x, recv_grad = (
        lax.all_to_all(
            lax.all_to_all(
                x_buf.reshape(capacity, EXPERTS, model_width),
                "dp",
                split_axis=2,
                concat_axis=0,
                tiled=True,
            ),
            "expert",
            split_axis=1,
            concat_axis=1,
            tiled=True,
        ),
        lax.all_to_all(
            lax.all_to_all(
                grad_buf.reshape(capacity, EXPERTS, model_width),
                "dp",
                split_axis=2,
                concat_axis=0,
                tiled=True,
            ),
            "expert",
            split_axis=1,
            concat_axis=1,
            tiled=True,
        ),
    )
    local_experts = w_gate.shape[0]
    sources = EXPERTS // local_experts
    rows_all = recv_x.shape[0]
    slice_width = recv_x.shape[2]
    token_rows = recv_x.reshape(rows_all, sources, local_experts, slice_width)
    grad_rows = recv_grad.reshape(rows_all, sources, local_experts, slice_width)
    pre_gate = jnp.einsum("cnld,ldf->cnlf", token_rows, w_gate, preferred_element_type=jnp.float32)
    pre_up = jnp.einsum("cnld,ldf->cnlf", token_rows, w_up, preferred_element_type=jnp.float32)
    grad_hidden = jnp.einsum(
        "cnld,lfd->cnlf", grad_rows, w_down, preferred_element_type=jnp.float32
    )
    partial_terms = lax.psum(jnp.stack([pre_gate, pre_up, grad_hidden], 3), "dp")
    hidden, gate_delta, up_delta = swiglu_back(
        partial_terms[:, :, :, 0], partial_terms[:, :, :, 1], partial_terms[:, :, :, 2]
    )
    grad_down = jnp.einsum(
        "cnlf,cnld->lfd", hidden, grad_rows, preferred_element_type=jnp.float32
    ).astype(jnp.bfloat16)
    grad_gate = jnp.einsum(
        "cnld,cnlf->ldf", token_rows, gate_delta, preferred_element_type=jnp.float32
    ).astype(jnp.bfloat16)
    grad_up = jnp.einsum(
        "cnld,cnlf->ldf", token_rows, up_delta, preferred_element_type=jnp.float32
    ).astype(jnp.bfloat16)
    row_grad = jnp.einsum("cnlf,ldf->cnld", gate_delta, w_gate, preferred_element_type=jnp.float32)
    row_grad = row_grad + jnp.einsum(
        "cnlf,ldf->cnld", up_delta, w_up, preferred_element_type=jnp.float32
    )
    table_float = table_sum.astype(jnp.float32)
    back_rows = lax.all_to_all(
        lax.all_to_all(
            row_grad.reshape(rows_all, EXPERTS, slice_width),
            "dp",
            split_axis=0,
            concat_axis=2,
            tiled=True,
        ),
        "expert",
        split_axis=1,
        concat_axis=1,
        tiled=True,
    )
    token_part = jnp.dot(
        table_float.T,
        back_rows.reshape(capacity * EXPERTS, model_width),
        precision=lax.Precision.HIGHEST,
        preferred_element_type=jnp.float32,
    )
    token_grad = lax.psum_scatter(token_part, "tensor", scatter_dimension=0, tiled=True)
    return (token_grad.astype(jnp.bfloat16), grad_gate, grad_up, grad_down)


def solution(mesh):
    placed = (
        P(("dp", "expert", "tensor"), None),
        P(("dp", "expert", "tensor"), None),
        P(("dp", "expert"), None),
        P(("dp", "expert"), None),
        P(("dp", "expert"), None),
        P("expert", "dp", "tensor"),
        P("expert", "dp", "tensor"),
        P("expert", "tensor", "dp"),
    )
    return jax.shard_map(
        shards,
        mesh=mesh,
        in_specs=placed,
        out_specs=(
            P(("dp", "expert", "tensor"), None),
            P("expert", "dp", "tensor"),
            P("expert", "dp", "tensor"),
            P("expert", "tensor", "dp"),
        ),
        check_vma=False,
    )
```

profile of v0, /device:TPU:0, one launch (start us, length us, event | category | flops | bytes accessed | tf_op | source)
XLA Modules:
  0.0 552.5 jit_solution(11450210532100585577)
XLA Ops:
  7.9 7.4 %all_gather.6 = bf16[32,4096]{1,0:T(8,128)(2,1)S(1)} all-gather(bf16[8,4096]{1,0:T(8,128)(2,1)} %param.8), channel_id=1, replica_groups=mesh['dp'=4,'expert'=2,'tensor'=4] {'tensor'}, dimensions={0}, use_global_device_ids=true | all-gather | bytes 327680 | tf_op jit(solution)/shard_map/all_gather | solution.py:30
  15.6 7.5 %copy.72 = bf16[10,8,4096]{0,1,2:T(8,128)(2,1)} copy(bf16[10,8,4096]{2,1,0:T(8,128)(2,1)S(1)} %fusion.11) | data formatting | bytes 1310720 | tf_op jit(solution)/shard_map/reshape | solution.py:47
  23.1 18.2 %reshape.43 = bf16[4,2,40960]{2,1,0:T(2,128)(2,1)} reshape(bf16[4096,8,10]{2,1,0:T(8,128)(2,1)} %bitcast.112) | data formatting | bytes 1310720
  41.3 4.9 all-to-all-start
  46.2 5.8 %all_gather.7 = bf16[32,4096]{1,0:T(8,128)(2,1)S(1)} all-gather(bf16[8,4096]{1,0:T(8,128)(2,1)S(1)} %copy-done.1), channel_id=1, replica_groups=mesh['dp'=4,'expert'=2,'tensor'=4] {'tensor'}, dimensions={0}, use_global_device_ids=true | all-gather | bytes 327680 | tf_op jit(solution)/shard_map/all_gather | solution.py:31
  52.8 7.5 %copy.78 = bf16[10,8,4096]{0,1,2:T(8,128)(2,1)} copy(bf16[10,8,4096]{2,1,0:T(8,128)(2,1)S(1)} %fusion.12) | data formatting | bytes 1310720 | tf_op jit(solution)/shard_map/reshape | solution.py:60
  60.2 18.2 %reshape.41 = bf16[4,2,40960]{2,1,0:T(2,128)(2,1)} reshape(bf16[4096,8,10]{2,1,0:T(8,128)(2,1)} %bitcast.113) | data formatting | bytes 1310720
  78.4 5.6 %all-to-all-start.2 = ((bf16[4,2,40960]{2,1,0:T(2,128)(2,1)}), bf16[4,2,40960]{2,1,0:T(2,128)(2,1)S(1)}, u32[]{:S(2)}, u32[]{:S(2)}) async-start(bf16[4,2,40960]{2,1,0:T(2,128)(2,1)} %reshape.41), calls=%async_computation.2 | async-start | bytes 1310720 | tf_op jit(solution)/shard_map/all_to_all | solution.py:59
  84.0 19.8 %reshape.44 = bf16[4096,8,10]{2,1,0:T(8,128)(2,1)} reshape(bf16[4,2,40960]{2,1,0:T(2,128)(2,1)S(1)} %all-to-all-done) | data formatting | bytes 1310720
  103.8 9.1 %copy.95 = bf16[10,8,4,1024]{3,2,1,0:T(4,128)(2,1)S(1)} copy(bf16[10,8,4,1024]{0,1,3,2:T(8,128)(2,1)} %bitcast.114) | data formatting | bytes 1310720 | tf_op jit(solution)/shard_map/all_to_all | solution.py:46
  117.8 19.8 %reshape.42 = bf16[4096,8,10]{2,1,0:T(8,128)(2,1)} reshape(bf16[4,2,40960]{2,1,0:T(2,128)(2,1)S(1)} %all-to-all-done.2) | data formatting | bytes 1310720
  137.6 9.1 %copy.96 = bf16[10,8,4,1024]{3,2,1,0:T(4,128)(2,1)S(1)} copy(bf16[10,8,4,1024]{0,1,3,2:T(8,128)(2,1)} %bitcast.115) | data formatting | bytes 1310720 | tf_op jit(solution)/shard_map/all_to_all | solution.py:59
  152.6 7.7 %fusion.13 = f32[40,2,4,1,1792]{4,0,1,2,3:T(8,128)S(1)} fusion(bf16[4,1024,1792]{2,1,0:T(8,128)(2,1)} %param.14, bf16[40,2,4,1024]{3,0,2,1:T(8,128)(2,1)S(1)} %bitcast.116), kind=kOutput, calls=%fused_computation.19 | convolution fusion | flops 1174405120 | bytes 17629184 | tf_op jit(solution)/shard_map/cnld,ldf->cnlf/dot_general | solution.py:79
  160.4 9.1 %fusion.16 = f32[40,2,4,1,1792]{4,0,1,2,3:T(8,128)} fusion(bf16[4,1024,1792]{2,1,0:T(8,128)(2,1)} %param.13, bf16[40,2,4,1024]{3,0,2,1:T(8,128)(2,1)S(1)} %bitcast.117), kind=kOutput, calls=%fused_computation.20 | convolution fusion | flops 1174405120 | bytes 17629184 | tf_op jit(solution)/shard_map/cnld,ldf->cnlf/dot_general | solution.py:78
  169.5 10.1 %fusion.19 = f32[40,2,4,1,1792]{4,0,1,2,3:T(8,128)S(1)} fusion(bf16[4,1792,1024]{2,1,0:T(8,128)(2,1)} %param.15, bf16[40,2,4,1024]{3,0,2,1:T(8,128)(2,1)} %bitcast.21), kind=kOutput, calls=%fused_computation.21 | convolution fusion | flops 1174405120 | bytes 17629184 | tf_op jit(solution)/shard_map/cnld,lfd->cnlf/dot_general | solution.py:80
  183.1 244.0 %all-reduce.2.cloned.1.call-done = f32[40,2,4,3,1792]{4,0,1,2,3:T(8,128)} async-done(((f32[40,2,4,3,1792]{4,0,1,2,3:T(8,128)}), f32[40,2,4,3,1792]{4,0,1,2,3:T(8,128)}) %all-reduce.2.cloned.1.call-update) | async-done | bytes 6881296 | tf_op jit(solution)/shard_map/psum | solution.py:83
  431.3 9.7 %fusion.2 = f32[4,40,2,1024]{3,1,2,0:T(8,128)S(1)} fusion(bf16[40,2,4,1792]{3,0,1,2:T(8,128)(2,1)S(1)} %get-tuple-element.5, bf16[4,1024,1792]{2,1,0:T(8,128)(2,1)} %param.13), kind=kOutput, calls=%fused_computation.5 | convolution fusion | flops 1174405120 | bytes 17137664 | tf_op jit(solution)/shard_map/cnlf,ldf->cnld/dot_general | solution.py:96
  441.0 9.9 %fusion.26 = f32[40,2,4,1024]{3,0,1,2:T(8,128)S(1)} fusion(f32[4,40,2,1024]{3,1,2,0:T(8,128)S(1)} %fusion.2, bf16[40,2,4,1792]{3,0,1,2:T(8,128)(2,1)S(1)} %get-tuple-element.4, bf16[4,1024,1792]{2,1,0:T(8,128)(2,1)} %param.14), kind=kOutput, calls=%fused_computation.31 | convolution fusion | flops 1174732800 | bytes 18448384 | tf_op jit(solution)/shard_map/cnlf,ldf->cnld/dot_general | solution.py:97
  451.8 33.9 %all_to_all.69 = f32[40,8,1024]{2,1,0:T(8,128)S(1)} all-to-all(f32[40,8,1024]{2,1,0:T(8,128)S(1)} %copy.84), channel_id=1, replica_groups=mesh['dp'=4,'expert'=2,'tensor'=4] {'dp'}, dimensions={0} | all-to-all | bytes 2621440 | tf_op jit(solution)/shard_map/all_to_all | solution.py:102
  495.5 12.0 %bitcast_convert_fusion = bf16[4,1792,1024]{2,1,0:T(8,128)(2,1)} fusion(f32[40,2,4,3,1792]{4,0,1,2,3:T(8,128)} %all-reduce.2.cloned.1.call-done, bf16[40,2,4,1024]{3,0,2,1:T(8,128)(2,1)} %bitcast.21), kind=kOutput, calls=%fused_computation | convolution fusion | flops 1185185792 | bytes 19922944 | tf_op jit(solution)/shard_map/cnlf,cnld->lfd/dot_general | solution.py:87
  507.5 12.5 %all-to-all-done.5 = f32[10,8,4096]{2,0,1:T(8,128)} async-done(((f32[10,8,4096]{2,0,1:T(8,128)}), f32[10,8,4096]{2,0,1:T(8,128)}, u32[]{:S(2)}, u32[]{:S(2)}) %all-to-all-start.5) | async-done | bytes 1310752 | tf_op jit(solution)/shard_map/all_to_all | solution.py:101
  523.6 7.6 %bitcast_convert_fusion.1 = bf16[4,1024,1792]{2,1,0:T(8,128)(2,1)} fusion(bf16[40,2,4,1024]{3,0,2,1:T(8,128)(2,1)S(1)} %bitcast.118, bf16[40,2,4,1792]{3,0,1,2:T(8,128)(2,1)S(1)} %get-tuple-element.4), kind=kOutput, calls=%fused_computation.1 | convolution fusion | flops 1181745152 | bytes 16482304 | tf_op jit(solution)/shard_map/cnld,cnlf->ldf/dot_general | solution.py:93
  531.2 7.6 %bitcast_convert_fusion.2 = bf16[4,1024,1792]{2,1,0:T(8,128)(2,1)} fusion(bf16[40,2,4,1024]{3,0,2,1:T(8,128)(2,1)S(1)} %bitcast.119, bf16[40,2,4,1792]{3,0,1,2:T(8,128)(2,1)S(1)} %get-tuple-element.5), kind=kOutput, calls=%fused_computation.2 | convolution fusion | flops 1181745152 | bytes 16482304 | tf_op jit(solution)/shard_map/cnld,cnlf->ldf/dot_general | solution.py:90
  538.8 5.0 reduce-scatter.2.cloned.1.call-done
  (35 shorter events, 36.2 us)
Async XLA Ops:
  23.1 23.1 %copy-start.1 = (bf16[8,4096]{1,0:T(8,128)(2,1)S(1)}, bf16[8,4096]{1,0:T(8,128)(2,1)}, u32[]{:S(2)}) copy-start(bf16[8,4096]{1,0:T(8,128)(2,1)} %param.9) | copy-start | bytes 196612
  23.1 28.8 %copy-start.2 = (f32[32,2]{0,1:T(2,128)S(1)}, f32[32,2]{0,1:T(2,128)}, u32[]{:S(2)}) copy-start(f32[32,2]{0,1:T(2,128)} %param.10) | copy-start | bytes 772
  41.3 37.1 %all-to-all-start = ((bf16[4,2,40960]{2,1,0:T(2,128)(2,1)}), bf16[4,2,40960]{2,1,0:T(2,128)(2,1)S(1)}, u32[]{:S(2)}, u32[]{:S(2)}) async-start(bf16[4,2,40960]{2,1,0:T(2,128)(2,1)} %reshape.43), calls=%async_computation | async-start | bytes 1310720 | tf_op jit(solution)/shard_map/all_to_all | solution.py:46
  78.4 35.9 %all-to-all-start.2 = ((bf16[4,2,40960]{2,1,0:T(2,128)(2,1)}), bf16[4,2,40960]{2,1,0:T(2,128)(2,1)S(1)}, u32[]{:S(2)}, u32[]{:S(2)}) async-start(bf16[4,2,40960]{2,1,0:T(2,128)(2,1)} %reshape.41), calls=%async_computation.2 | async-start | bytes 1310720 | tf_op jit(solution)/shard_map/all_to_all | solution.py:59
  114.3 33.8 %all-to-all-start.1 = ((bf16[40,8,1024]{2,0,1:T(8,128)(2,1)}), bf16[40,8,1024]{2,0,1:T(8,128)(2,1)S(1)}, u32[]{:S(2)}, u32[]{:S(2)}) async-start(bf16[40,8,1024]{2,0,1:T(8,128)(2,1)} %copy.75), calls=%async_computation.1 | async-start | bytes 1310720 | tf_op jit(solution)/shard_map/all_to_all | solution.py:45
  148.1 21.4 %all-to-all-start.3 = ((bf16[40,8,1024]{2,0,1:T(8,128)(2,1)}), bf16[40,8,1024]{2,0,1:T(8,128)(2,1)}, u32[]{:S(2)}, u32[]{:S(2)}) async-start(bf16[40,8,1024]{2,0,1:T(8,128)(2,1)} %copy.81), calls=%async_computation.3 | async-start | bytes 1310720 | tf_op jit(solution)/shard_map/all_to_all | solution.py:58
  152.4 274.8 %all-reduce.2.cloned.1.call-start = ((), (), s32[]{:S(2)}) async-start(), calls=%async_computation.7 | async-start | bytes 13762560 | tf_op jit(solution)/shard_map/psum | solution.py:83
  169.5 10.1 %copy-start = (f32[40,2,4,1,1792]{4,0,1,2,3:T(8,128)S(1)}, f32[40,2,4,1,1792]{4,0,1,2,3:T(8,128)}, u32[]{:S(2)}) copy-start(f32[40,2,4,1,1792]{4,0,1,2,3:T(8,128)} %fusion.16) | copy-start | bytes 6881284
  490.6 29.3 %all-to-all-start.5 = ((f32[10,8,4096]{2,0,1:T(8,128)}), f32[10,8,4096]{2,0,1:T(8,128)}, u32[]{:S(2)}, u32[]{:S(2)}) async-start(f32[10,8,4096]{2,0,1:T(8,128)} %reshape.40), calls=%async_computation.5 | async-start | bytes 4194304 | tf_op jit(solution)/shard_map/all_to_all | solution.py:101
  495.4 48.3 %reduce-scatter.2.cloned.1.call-start = ((), (), s32[]{:S(2)}) async-start(), calls=%async_computation.8 | async-start | bytes 655360 | tf_op jit(solution)/shard_map/reduce_scatter | solution.py:120
Sparse Core Ops, SparseCore 0:
  183.2 243.8 all-reduce.1
  523.7 20.0 reduce-scatter.1
where the time goes:
time: 561 us; the launch traced here: 553 us
  waiting for transfers between devices  262 us (47%)
  local copies, waits for them, and re-layouts  118 us (21%)
  matrix products  78.4 us (14%)
  blocking collectives  47.1 us (8%)
  starting transfers between devices  23.3 us (4%)
  between operations  14.5 us (3%)
  other arithmetic  9.94 us (2%)
    psum x1, waiting for transfers between devices, shards(): lax.psum(jnp.stack([pre_gate, pre_up, grad_hidden], 3), 'dp')  244 us
    unnamed x10, local copies, waits for them, and re-layouts  76 us
    all_to_all x1, blocking collectives, shards(): lax.all_to_all(row_grad.reshape(rows_all, EXPERTS, slice_width), 'dp', sp...  33.9 us
    all_to_all x1, waiting for transfers between devices, shards(): lax.all_to_all(lax.all_to_all(row_grad.reshape(rows_all, EXPERTS, slice_w...  12.5 us
    dot_general x1, matrix products, shards(): jnp.einsum('cnlf,cnld->lfd', hidden, grad_rows, preferred_element_type=jn...  12 us
  transfers between devices with their start and end apart: 7, of which 3 were waited for; matrix products, arithmetic and copies ran while one was open for 24% of the time, Pallas kernels for 0%

commit v1 on v0

v1 whole, which is shorter than its diff:
```python
import jax
import jax.numpy as jnp
from jax import lax
from jax.sharding import PartitionSpec as P

EXPERTS = 8
TOP = 2
LANES = 128
F32 = jnp.float32
BF16 = jnp.bfloat16


def swiglu_back(pre_gate, pre_up, grad_hidden):
    sigmoid_gate = jax.nn.sigmoid(pre_gate)
    silu_gate = pre_gate * sigmoid_gate
    hidden = (silu_gate * pre_up).astype(BF16)
    up_delta = (grad_hidden * silu_gate).astype(BF16)
    gate_delta = (
        grad_hidden * pre_up * sigmoid_gate * (1.0 + pre_gate * (1.0 - sigmoid_gate))
    ).astype(BF16)
    return (hidden, gate_delta, up_delta)


def strides(n):
    return [1 << k for k in range(n.bit_length() - 1)]


def swap(value, n, stride):
    return lax.ppermute(value, "dp", [(i, i ^ stride) for i in range(n)])


def sum_rows(partial):
    n = lax.axis_size("dp")
    at = lax.axis_index("dp")
    part = partial
    for stride in strides(n):
        half = part.shape[0] // 2
        bit = (at // stride) % 2
        keep = lax.dynamic_slice_in_dim(part, bit * half, half, 0)
        send = lax.dynamic_slice_in_dim(part, (1 - bit) * half, half, 0)
        part = keep.astype(F32) + swap(send.astype(BF16), n, stride).astype(F32)
        if 2 * stride < n:
            part = part.astype(BF16)
    return part


def all_rows(first, others, work):
    n = lax.axis_size("dp")
    at = lax.axis_index("dp")

    def grow(own, stride):
        other = swap(own, n, stride)
        low = (at // stride) % 2 == 0
        whole = jnp.concatenate([jnp.where(low, own, other), jnp.where(low, other, own)], 0)
        return other, whole

    steps = list(reversed(strides(n)))
    arrays = [first] + list(others)
    for k in range(len(arrays)):
        for step, stride in enumerate(steps):
            if k > 1 and step == len(steps) - 1:
                arrays[k], back = lax.optimization_barrier((arrays[k], done[0]))
                done = (back,) + done[1:]
            other, arrays[k] = grow(arrays[k], stride)
            if step == 0 and k + 1 < len(arrays):
                arrays[k + 1], arrays[k] = lax.optimization_barrier((arrays[k + 1], arrays[k]))
        if k == 0:
            done = work(arrays[0])
    return arrays, done


def shards(tokens, out_grad, route_probs, expert_ids, slot_index, w_gate, w_up, w_down):
    dp = lax.axis_size("dp")
    ex = lax.axis_size("expert")
    tn = lax.axis_size("tensor")
    held, model_width = tokens.shape
    block_rows = held * tn
    blocks = dp * ex
    capacity = 5 * block_rows * TOP // (4 * EXPERTS)
    local_experts, slice_width, hidden_width = w_gate.shape
    token_count = blocks * block_rows
    rows = blocks * capacity
    places = local_experts * rows

    mine = lax.axis_index("tensor") * held

    def own_rows(routes):
        return lax.dynamic_slice_in_dim(routes, mine, held, 0)

    pieces, left = [], own_rows(route_probs)
    for _ in range(3):
        piece = lax.reduce_precision(left, 8, 7)
        pieces.append(piece)
        left = left - piece
    info = [own_rows(expert_ids).astype(F32), own_rows(slot_index).astype(F32)] + pieces
    info = jnp.concatenate(info, 1).astype(BF16)
    info = jnp.pad(info, ((0, 0), (0, LANES - info.shape[1])))
    both = jnp.concatenate(
        [
            tokens.reshape(held, dp, slice_width),
            jnp.broadcast_to(info[:, None, :], (held, dp, LANES)),
            out_grad.reshape(held, dp, slice_width),
        ],
        2,
    )
    both = lax.all_to_all(
        jnp.moveaxis(both, 1, 0), "dp", split_axis=0, concat_axis=0, tiled=True
    ).reshape(dp * held, 2 * slice_width + LANES)
    first = lax.all_gather(
        both[:, : slice_width + LANES], ("expert", "tensor"), axis=0, tiled=True
    )
    own_dy = both[:, slice_width + LANES :]
    all_x = first[:, :slice_width]
    info = first[:, slice_width : slice_width + 5 * TOP].astype(F32).reshape(token_count, 5, TOP)
    ids = info[:, 0].astype(jnp.int32).T
    slots = info[:, 1].astype(jnp.int32).T
    probs = ((info[:, 2] + info[:, 3]) + info[:, 4]).T
    block = lax.broadcasted_iota(jnp.int32, (ex, tn, dp, held), 2) * ex
    block = (block + lax.broadcasted_iota(jnp.int32, (ex, tn, dp, held), 0)).reshape(token_count)
    local = ids - lax.axis_index("expert") * local_experts
    kept = (slots < capacity) & (local >= 0) & (local < local_experts)
    target = jnp.where(kept, local * rows + block[None, :] * capacity + slots, -1)
    place = jnp.arange(places, dtype=jnp.int32)
    tables = [(place[:, None] == target[k][None, :]).astype(BF16) for k in range(TOP)]
    table_sum = tables[0] + tables[1]

    x_rows = jnp.dot(table_sum, all_x, preferred_element_type=F32).astype(BF16)
    x_exp = x_rows.reshape(local_experts, rows, slice_width)

    def flat(value):
        return value.astype(BF16).reshape(places, hidden_width)

    def per_expert(value):
        return value.reshape(local_experts, rows, hidden_width)

    part_gate = flat(jnp.einsum("lrd,ldf->lrf", x_exp, w_gate, preferred_element_type=F32))
    own_dy, part_gate = lax.optimization_barrier((own_dy, part_gate))
    pre_gate = sum_rows(part_gate)
    all_dy = lax.all_gather(own_dy, ("expert", "tensor"), axis=0, tiled=True)
    scaled = [(probs[k][:, None] * all_dy.astype(F32)).astype(BF16) for k in range(TOP)]
    g_rows = jnp.dot(
        jnp.concatenate(tables, 1), jnp.concatenate(scaled, 0), preferred_element_type=F32
    ).astype(BF16)
    g_exp = g_rows.reshape(local_experts, rows, slice_width)

    pre_up = sum_rows(flat(jnp.einsum("lrd,ldf->lrf", x_exp, w_up, preferred_element_type=F32)))
    grad_hidden = sum_rows(
        flat(jnp.einsum("lrd,lfd->lrf", g_exp, w_down, preferred_element_type=F32))
    )
    hidden, gate_delta, up_delta = swiglu_back(pre_gate, pre_up, grad_hidden)
    def gate_work(rows_all):
        delta = per_expert(rows_all)
        back = jnp.einsum("lrf,ldf->lrd", delta, w_gate, preferred_element_type=F32)
        grad = jnp.einsum("lrd,lrf->ldf", x_exp, delta, preferred_element_type=F32)
        return back, grad.astype(BF16)

    arrays, (row_grad, grad_gate) = all_rows(gate_delta, (up_delta, hidden), gate_work)
    up_delta, hidden = per_expert(arrays[1]), per_expert(arrays[2])
    up_delta, row_grad = lax.optimization_barrier((up_delta, row_grad))
    row_grad = row_grad + jnp.einsum("lrf,ldf->lrd", up_delta, w_up, preferred_element_type=F32)
    grad_up = jnp.einsum("lrd,lrf->ldf", x_exp, up_delta, preferred_element_type=F32)
    grad_down = jnp.einsum("lrf,lrd->lfd", hidden, g_exp, preferred_element_type=F32)

    token_part = jnp.dot(
        table_sum.astype(F32).T,
        row_grad.reshape(places, slice_width),
        precision=lax.Precision.HIGHEST,
        preferred_element_type=F32,
    )
    parts = lax.all_to_all(
        token_part.astype(BF16).reshape(ex * tn, dp * held, slice_width),
        ("expert", "tensor"),
        split_axis=0,
        concat_axis=0,
        tiled=True,
    )
    token_grad = jnp.sum(parts.astype(F32), 0).astype(BF16)
    token_grad = lax.all_to_all(
        token_grad.reshape(dp, held, slice_width), "dp", split_axis=0, concat_axis=0, tiled=True
    )
    token_grad = jnp.moveaxis(token_grad, 0, 1).reshape(held, model_width)
    return (token_grad, grad_gate, grad_up.astype(BF16), grad_down.astype(BF16))


def solution(mesh):
    rows = P(("dp", "expert", "tensor"), None)
    routes = P(("dp", "expert"), None)
    wide = P("expert", "dp", "tensor")
    tall = P("expert", "tensor", "dp")
    return jax.shard_map(
        shards,
        mesh=mesh,
        in_specs=(rows, rows, routes, routes, routes, wide, wide, tall),
        out_specs=(rows, wide, wide, tall),
        check_vma=False,
    )
```

time: 561 us -> 203 us (0.36); the launches traced: 553 us -> 202 us
  waiting for transfers between devices: 262 us -> 79.8 us
  local copies, waits for them, and re-layouts: 118 us -> 2.94 us
  blocking collectives: 47.1 us -> 20 us
  between operations: 14.5 us -> 0.93 us
  matrix products: 78.4 us -> 65.3 us
    psum x1 -> x0, waiting for transfers between devices: 244 us -> none  [shards(): lax.psum(jnp.stack([pre_gate, pre_up, grad_hidden], 3), 'dp')]
    unnamed x10 -> x7, local copies, waits for them, and re-layouts: 76 us -> 1.09 us
    ppermute x0 -> x12, waiting for transfers between devices: none -> 73.9 us  [swap(): return lax.ppermute(value, 'dp', [(i, i ^ stride) for i in range(n)])]
    all_to_all x1 -> x0, blocking collectives: 33.9 us -> none  [shards(): lax.all_to_all(row_grad.reshape(rows_all, EXPERTS, slice_width), 'dp', sp...]
    all_to_all x8 -> x0, local copies, waits for them, and re-layouts: 25.9 us -> none  [the longest x3 10.5 us: shards(): lax.all_to_all(x_buf.reshape(capacity, EXPERTS, model_width), 'dp', split...]
    reshape x3 -> x1, local copies, waits for them, and re-layouts: 15.7 us -> 0.02 us  [shards(): first[:, slice_width:slice_width + 5 * TOP].astype(F32)]
    dot_general x12 -> x11, matrix products: 78.4 us -> 65.3 us  [the longest x1 9.71 us: shards(): jnp.einsum('lrd,lfd->lrf', g_exp, w_down, preferred_element_type=F32)]
    ppermute x0 -> x12, starting transfers between devices: none -> 10.3 us  [swap(): return lax.ppermute(value, 'dp', [(i, i ^ stride) for i in range(n)])]
  transfers between devices with their start and end apart: 7 -> 15, of which waited for: 3 -> 8; matrix products, arithmetic and copies ran while one was open for 24% -> 30% of each run, Pallas kernels for 0% -> 0%
where the time goes in v1:
time: 203 us; the launch traced here: 202 us
  waiting for transfers between devices  79.8 us (39%)
  matrix products  65.3 us (32%)
  starting transfers between devices  23.5 us (12%)
  blocking collectives  20 us (10%)
  other arithmetic  9.71 us (5%)
  local copies, waits for them, and re-layouts  2.94 us (1%)
    ppermute x12, waiting for transfers between devices, swap(): return lax.ppermute(value, 'dp', [(i, i ^ stride) for i in range(n)])  73.9 us
    ppermute x12, starting transfers between devices, swap(): return lax.ppermute(value, 'dp', [(i, i ^ stride) for i in range(n)])  10.3 us
    all_gather x1, blocking collectives, shards(): all_dy = lax.all_gather(own_dy, ('expert', 'tensor'), axis=0, tiled=True)  10 us
    all_gather x1, blocking collectives, shards(): lax.all_gather(both[:, :slice_width + LANES], ('expert', 'tensor'), axis=...  10 us
    dot_general x1, matrix products, shards(): jnp.einsum('lrd,lfd->lrf', g_exp, w_down, preferred_element_type=F32)  9.71 us
    dot_general x1, matrix products, shards(): jnp.einsum('lrf,ldf->lrd', up_delta, w_up, preferred_element_type=F32)  9.69 us
    dot_general x1, matrix products, gate_work(): back = jnp.einsum('lrf,ldf->lrd', delta, w_gate, preferred_element_type=F32)  9.68 us
    dot_general x1, matrix products, shards(): jnp.einsum('lrd,ldf->lrf', x_exp, w_up, preferred_element_type=F32)  7.86 us
  transfers between devices with their start and end apart: 15, of which 8 were waited for; matrix products, arithmetic and copies ran while one was open for 30% of the time, Pallas kernels for 0%

profile of v1, /device:TPU:0, one launch (start us, length us, event | category | flops | bytes accessed | tf_op | source)
XLA Modules:
  0.0 202.2 jit_solution(3145310261565313127)
XLA Ops:
  3.9 6.3 %all-to-all-start = ((bf16[4,8,2176]{2,1,0:T(8,128)(2,1)}), bf16[4,8,2176]{2,1,0:T(8,128)(2,1)S(1)}, u32[]{:S(2)}, u32[]{:S(2)}) async-start(bf16[4,8,2176]{2,1,0:T(8,128)(2,1)} %maximum_bitcast_fusion), calls=%async_computation | async-start | bytes 278528 | tf_op jit(solution)/shard_map/all_to_all | solution.py:106
  10.4 6.0 %all-to-all-done = bf16[4,8,2176]{2,1,0:T(8,128)(2,1)S(1)} async-done(((bf16[4,8,2176]{2,1,0:T(8,128)(2,1)}), bf16[4,8,2176]{2,1,0:T(8,128)(2,1)S(1)}, u32[]{:S(2)}, u32[]{:S(2)}) %all-to-all-start) | async-done | bytes 139296 | tf_op jit(solution)/shard_map/all_to_all | solution.py:106
  16.4 10.0 %all_gather.6 = bf16[256,1152]{1,0:T(8,128)(2,1)S(1)} all-gather(bf16[32,1152]{1,0:T(8,128)(2,1)S(1)} %slice.52), channel_id=1, replica_groups=mesh['dp'=4,'expert'=2,'tensor'=4] {'expert','tensor'}, dimensions={0}, use_global_device_ids=true | all-gather | bytes 663552 | tf_op jit(solution)/shard_map/all_gather | solution.py:109
  27.0 7.9 %convolution_convert_fusion.4 = bf16[4,80,1792]{2,1,0:T(8,128)(2,1)S(1)} fusion(bf16[4,80,1024]{2,1,0:T(8,128)(2,1)S(1)} %bitcast.78, bf16[4,1024,1792]{2,1,0:T(8,128)(2,1)} %param.14), kind=kOutput, calls=%fused_computation.4 | convolution fusion | flops 1174978560 | bytes 16482304 | tf_op jit(solution)/shard_map/lrd,ldf->lrf/dot_general | solution.py:146
  36.4 2.6 %convolution_convert_fusion.5 = bf16[4,80,1792]{2,1,0:T(8,128)(2,1)S(1)} fusion(bf16[4,80,1024]{2,1,0:T(8,128)(2,1)S(1)} %bitcast.79, bf16[4,1024,1792]{2,1,0:T(8,128)(2,1)S(1)} %copy-done), kind=kOutput, calls=%fused_computation.5 | convolution fusion | flops 1174978560 | bytes 16482304 | tf_op jit(solution)/shard_map/lrd,ldf->lrf/dot_general | solution.py:136
  38.9 10.0 %all_gather.7 = bf16[256,1024]{1,0:T(8,128)(2,1)S(1)} all-gather(bf16[32,1024]{1,0:T(8,128)(2,1)S(1)} %slice.58), channel_id=1, replica_groups=mesh['dp'=4,'expert'=2,'tensor'=4] {'expert','tensor'}, dimensions={0}, use_global_device_ids=true | all-gather | bytes 589824 | tf_op jit(solution)/shard_map/all_gather | solution.py:139
  50.9 9.7 %convolution_convert_fusion.3 = bf16[4,80,1792]{2,1,0:T(8,128)(2,1)S(1)} fusion(bf16[4,80,1024]{2,1,0:T(8,128)(2,1)S(1)} %bitcast.86, bf16[4,1792,1024]{2,1,0:T(8,128)(2,1)} %param.15), kind=kOutput, calls=%fused_computation.3 | convolution fusion | flops 1174978560 | bytes 16482304 | tf_op jit(solution)/shard_map/lrd,lfd->lrf/dot_general | solution.py:148
  62.6 2.3 %collective-permute-done = bf16[160,1792]{1,0:T(8,128)(2,1)S(1)} collective-permute-done((bf16[160,1792]{1,0:T(8,128)(2,1)S(1)}, bf16[160,1792]{1,0:T(8,128)(2,1)S(1)}, u32[]{:S(2)}, u32[]{:S(2)}) %collective-permute-start) | collective-permute-done | bytes 573472 | tf_op jit(solution)/shard_map/ppermute | solution.py:29
  66.5 21.7 %collective-permute-done.4 = bf16[160,1792]{1,0:T(8,128)(2,1)S(1)} collective-permute-done((bf16[160,1792]{1,0:T(8,128)(2,1)S(1)}, bf16[160,1792]{1,0:T(8,128)(2,1)S(1)}, u32[]{:S(2)}, u32[]{:S(2)}) %collective-permute-start.4) | collective-permute-done | bytes 573472 | tf_op jit(solution)/shard_map/ppermute | solution.py:29
  89.9 14.3 %collective-permute-done.5 = bf16[80,1792]{1,0:T(8,128)(2,1)} collective-permute-done((bf16[80,1792]{1,0:T(8,128)(2,1)}, bf16[80,1792]{1,0:T(8,128)(2,1)}, u32[]{:S(2)}, u32[]{:S(2)}) %collective-permute-start.5) | collective-permute-done | bytes 286752 | tf_op jit(solution)/shard_map/ppermute | solution.py:29
  104.2 2.4 %multiply_convert_fusion = (bf16[80,1792]{1,0:T(8,128)(2,1)}, bf16[80,1792]{1,0:T(8,128)(2,1)}, bf16[80,1792]{1,0:T(8,128)(2,1)S(1)}) fusion(bf16[80,1792]{1,0:T(8,128)(2,1)} %collective-permute-done.1, bf16[80,1792]{1,0:T(8,128)(2,1)} %collective-permute-done.3, bf16[80,1792]{1,0:T(8,128)(2,1)} %collective-permute-done.5, ...), kind=kLoop, calls=%fused_computation.26 | loop fusion | flops 3440640 | bytes 2580484 | tf_op jit(solution)/shard_map/convert_element_type | solution.py:20
  106.6 15.1 %collective-permute-done.6 = bf16[80,1792]{1,0:T(8,128)(2,1)S(1)} collective-permute-done((bf16[80,1792]{1,0:T(8,128)(2,1)}, bf16[80,1792]{1,0:T(8,128)(2,1)S(1)}, u32[]{:S(2)}, u32[]{:S(2)}) %collective-permute-start.6) | collective-permute-done | bytes 286752 | tf_op jit(solution)/shard_map/ppermute | solution.py:29
  122.8 2.6 %collective-permute-start.10 = (bf16[160,1792]{1,0:T(8,128)(2,1)S(1)}, bf16[160,1792]{1,0:T(8,128)(2,1)S(1)}, u32[]{:S(2)}, u32[]{:S(2)}) collective-permute-start(bf16[160,1792]{1,0:T(8,128)(2,1)S(1)} %pad_maximum_fusion.3), channel_id=1, source_target_pairs={{0,8},{8,0},{16,24},{24,16},{1,9},{9,1},{17,25},{25,17},{2,10},{10... | collective-permute-start | bytes 1720328 | tf_op jit(solution)/shard_map/ppermute | solution.py:29
  125.5 12.7 %collective-permute-done.7 = bf16[80,1792]{1,0:T(8,128)(2,1)S(1)} collective-permute-done((bf16[80,1792]{1,0:T(8,128)(2,1)S(1)}, bf16[80,1792]{1,0:T(8,128)(2,1)S(1)}, u32[]{:S(2)}, u32[]{:S(2)}) %collective-permute-start.7) | collective-permute-done | bytes 286752 | tf_op jit(solution)/shard_map/ppermute | solution.py:29
  138.4 2.3 %collective-permute-start.8 = (bf16[160,1792]{1,0:T(8,128)(2,1)S(1)}, bf16[160,1792]{1,0:T(8,128)(2,1)S(1)}, u32[]{:S(2)}, u32[]{:S(2)}) collective-permute-start(bf16[160,1792]{1,0:T(8,128)(2,1)S(1)} %pad_maximum_fusion.4), channel_id=1, source_target_pairs={{0,8},{8,0},{16,24},{24,16},{1,9},{9,1},{17,25},{25,17},{2,10},{10... | collective-permute-start | bytes 1720328 | tf_op jit(solution)/shard_map/ppermute | solution.py:29
  140.6 7.3 %collective-permute-done.10 = bf16[160,1792]{1,0:T(8,128)(2,1)S(1)} collective-permute-done((bf16[160,1792]{1,0:T(8,128)(2,1)S(1)}, bf16[160,1792]{1,0:T(8,128)(2,1)S(1)}, u32[]{:S(2)}, u32[]{:S(2)}) %collective-permute-start.10) | collective-permute-done | bytes 573472 | tf_op jit(solution)/shard_map/ppermute | solution.py:29
  148.1 9.7 %fusion.32 = f32[4,80,1024]{2,1,0:T(8,128)S(1)} fusion(bf16[4,80,1792]{2,1,0:T(8,128)(2,1)S(1)} %bitcast.74, bf16[4,1024,1792]{2,1,0:T(8,128)(2,1)} %param.13), kind=kOutput, calls=%fused_computation.93 | convolution fusion | flops 1174405120 | bytes 17137664 | tf_op jit(solution)/shard_map/lrf,ldf->lrd/dot_general | solution.py:153
  157.9 7.8 %convolution_convert_fusion.2 = bf16[4,1024,1792]{2,1,0:T(8,128)(2,1)} fusion(bf16[4,80,1024]{2,1,0:T(8,128)(2,1)S(1)} %bitcast.80, bf16[4,80,1792]{2,1,0:T(8,128)(2,1)S(1)} %bitcast.75), kind=kOutput, calls=%fused_computation.2 | convolution fusion | flops 1181745152 | bytes 16482304 | tf_op jit(solution)/shard_map/lrd,lrf->ldf/dot_general | solution.py:154
  165.9 9.7 %convolution_add_fusion = f32[4,80,1024]{2,1,0:T(8,128)S(1)} fusion(f32[4,80,1024]{2,1,0:T(8,128)S(1)} %fusion.32, bf16[4,80,1792]{2,1,0:T(8,128)(2,1)S(1)} %bitcast.76, bf16[4,1024,1792]{2,1,0:T(8,128)(2,1)} %param.14), kind=kOutput, calls=%fused_computation.6 | convolution fusion | flops 1174732800 | bytes 18448384 | tf_op jit(solution)/shard_map/lrf,ldf->lrd/dot_general | solution.py:160
  175.6 2.0 convolution_convert_fusion.8
  177.6 3.5 %all-to-all-start.1 = ((bf16[8,32,1024]{2,1,0:T(8,128)(2,1)}), bf16[8,32,1024]{2,1,0:T(8,128)(2,1)S(1)}, u32[]{:S(2)}, u32[]{:S(2)}) async-start(bf16[8,32,1024]{2,1,0:T(8,128)(2,1)} %bitcast.92), calls=%async_computation.1 | async-start | bytes 1048576 | tf_op jit(solution)/shard_map/all_to_all | solution.py:170
  181.1 7.6 %convolution_convert_fusion.1 = bf16[4,1024,1792]{2,1,0:T(8,128)(2,1)} fusion(bf16[4,80,1024]{2,1,0:T(8,128)(2,1)S(1)} %bitcast.81, bf16[4,80,1792]{2,1,0:T(8,128)(2,1)S(1)} %bitcast.77), kind=kOutput, calls=%fused_computation.1 | convolution fusion | flops 1181745152 | bytes 16482304 | tf_op jit(solution)/shard_map/lrd,lrf->ldf/dot_general | solution.py:161
  190.6 3.3 %all-to-all-start.2 = ((bf16[4,8,1024]{2,1,0:T(8,128)(2,1)}), bf16[4,8,1024]{2,1,0:T(8,128)(2,1)S(1)}, u32[]{:S(2)}, u32[]{:S(2)}) async-start(bf16[4,8,1024]{2,1,0:T(8,128)(2,1)} %bitcast.25), calls=%async_computation.2 | async-start | bytes 131072 | tf_op jit(solution)/shard_map/all_to_all | solution.py:178
  194.0 7.6 %convolution_convert_fusion = bf16[4,1792,1024]{2,1,0:T(8,128)(2,1)} fusion(bf16[4,80,1792]{2,1,0:T(8,128)(2,1)S(1)} %bitcast.85, bf16[4,80,1024]{2,1,0:T(8,128)(2,1)S(1)} %bitcast.87), kind=kOutput, calls=%fused_computation | convolution fusion | flops 1181745152 | bytes 16482304 | tf_op jit(solution)/shard_map/lrf,lrd->lfd/dot_general | solution.py:162
  (69 shorter events, 17.1 us)
Async XLA Ops:
  3.9 12.5 %all-to-all-start = ((bf16[4,8,2176]{2,1,0:T(8,128)(2,1)}), bf16[4,8,2176]{2,1,0:T(8,128)(2,1)S(1)}, u32[]{:S(2)}, u32[]{:S(2)}) async-start(bf16[4,8,2176]{2,1,0:T(8,128)(2,1)} %maximum_bitcast_fusion), calls=%async_computation | async-start | bytes 278528 | tf_op jit(solution)/shard_map/all_to_all | solution.py:106
  27.0 9.4 %copy-start = (bf16[4,1024,1792]{2,1,0:T(8,128)(2,1)S(1)}, bf16[4,1024,1792]{2,1,0:T(8,128)(2,1)}, u32[]{:S(2)}) copy-start(bf16[4,1024,1792]{2,1,0:T(8,128)(2,1)} %param.13) | copy-start | bytes 44040196
  34.9 26.7 %collective-permute-start.2 = (bf16[160,1792]{1,0:T(8,128)(2,1)S(1)}, bf16[160,1792]{1,0:T(8,128)(2,1)S(1)}, u32[]{:S(2)}, u32[]{:S(2)}) collective-permute-start(bf16[160,1792]{1,0:T(8,128)(2,1)S(1)} %constant_dynamic-slice_fusion.3), channel_id=1, source_target_pairs={{0,8},{8,0},{16,24},{24,16},{1,9},{9,1},{17,25},{25,17},{2,10},{10... | collective-permute-start | bytes 1720328 | tf_op jit(solution)/shard_map/ppermute | solution.py:29
  49.0 15.9 %collective-permute-start = (bf16[160,1792]{1,0:T(8,128)(2,1)S(1)}, bf16[160,1792]{1,0:T(8,128)(2,1)S(1)}, u32[]{:S(2)}, u32[]{:S(2)}) collective-permute-start(bf16[160,1792]{1,0:T(8,128)(2,1)S(1)} %constant_dynamic-slice_fusion.5), channel_id=1, source_target_pairs={{0,8},{8,0},{16,24},{24,16},{1,9},{9,1},{17,25},{25,17},{2,10},{10... | collective-permute-start | bytes 1720328 | tf_op jit(solution)/shard_map/ppermute | solution.py:29
  60.7 27.5 %collective-permute-start.4 = (bf16[160,1792]{1,0:T(8,128)(2,1)S(1)}, bf16[160,1792]{1,0:T(8,128)(2,1)S(1)}, u32[]{:S(2)}, u32[]{:S(2)}) collective-permute-start(bf16[160,1792]{1,0:T(8,128)(2,1)S(1)} %constant_dynamic-slice_fusion.1), channel_id=1, source_target_pairs={{0,8},{8,0},{16,24},{24,16},{1,9},{9,1},{17,25},{25,17},{2,10},{10... | collective-permute-start | bytes 1720328 | tf_op jit(solution)/shard_map/ppermute | solution.py:29
  61.8 27.5 %collective-permute-start.3 = (bf16[80,1792]{1,0:T(8,128)(2,1)S(1)}, bf16[80,1792]{1,0:T(8,128)(2,1)}, u32[]{:S(2)}, u32[]{:S(2)}) collective-permute-start(bf16[80,1792]{1,0:T(8,128)(2,1)S(1)} %constant_dynamic-slice_fusion.2), channel_id=1, source_target_pairs={{0,16},{8,24},{16,0},{24,8},{1,17},{9,25},{17,1},{25,9},{2,18},{10... | collective-permute-start | bytes 860168 | tf_op jit(solution)/shard_map/ppermute | solution.py:29
  65.8 24.1 %collective-permute-start.1 = (bf16[80,1792]{1,0:T(8,128)(2,1)}, bf16[80,1792]{1,0:T(8,128)(2,1)}, u32[]{:S(2)}, u32[]{:S(2)}) collective-permute-start(bf16[80,1792]{1,0:T(8,128)(2,1)} %constant_dynamic-slice_fusion.4), channel_id=1, source_target_pairs={{0,16},{8,24},{16,0},{24,8},{1,17},{9,25},{17,1},{25,9},{2,18},{10... | collective-permute-start | bytes 860168 | tf_op jit(solution)/shard_map/ppermute | solution.py:29
  89.1 15.2 %collective-permute-start.5 = (bf16[80,1792]{1,0:T(8,128)(2,1)}, bf16[80,1792]{1,0:T(8,128)(2,1)}, u32[]{:S(2)}, u32[]{:S(2)}) collective-permute-start(bf16[80,1792]{1,0:T(8,128)(2,1)} %constant_dynamic-slice_fusion), channel_id=1, source_target_pairs={{0,16},{8,24},{16,0},{24,8},{1,17},{9,25},{17,1},{25,9},{2,18},{10... | collective-permute-start | bytes 860168 | tf_op jit(solution)/shard_map/ppermute | solution.py:29
  106.6 15.1 %collective-permute-start.6 = (bf16[80,1792]{1,0:T(8,128)(2,1)}, bf16[80,1792]{1,0:T(8,128)(2,1)S(1)}, u32[]{:S(2)}, u32[]{:S(2)}) collective-permute-start(bf16[80,1792]{1,0:T(8,128)(2,1)} %get-tuple-element.24), channel_id=1, source_target_pairs={{0,16},{8,24},{16,0},{24,8},{1,17},{9,25},{17,1},{25,9},{2,18},{10... | collective-permute-start | bytes 860168 | tf_op jit(solution)/shard_map/ppermute | solution.py:29
  106.6 16.1 %copy-start.1 = (bf16[80,1792]{1,0:T(8,128)(2,1)S(1)}, bf16[80,1792]{1,0:T(8,128)(2,1)}, u32[]{:S(2)}) copy-start(bf16[80,1792]{1,0:T(8,128)(2,1)} %get-tuple-element.16) | copy-start | bytes 860164
  122.8 15.4 %collective-permute-start.7 = (bf16[80,1792]{1,0:T(8,128)(2,1)S(1)}, bf16[80,1792]{1,0:T(8,128)(2,1)S(1)}, u32[]{:S(2)}, u32[]{:S(2)}) collective-permute-start(bf16[80,1792]{1,0:T(8,128)(2,1)S(1)} %copy-done.1), channel_id=1, source_target_pairs={{0,16},{8,24},{16,0},{24,8},{1,17},{9,25},{17,1},{25,9},{2,18},{10... | collective-permute-start | bytes 860168 | tf_op jit(solution)/shard_map/ppermute | solution.py:29
  122.8 25.1 %collective-permute-start.10 = (bf16[160,1792]{1,0:T(8,128)(2,1)S(1)}, bf16[160,1792]{1,0:T(8,128)(2,1)S(1)}, u32[]{:S(2)}, u32[]{:S(2)}) collective-permute-start(bf16[160,1792]{1,0:T(8,128)(2,1)S(1)} %pad_maximum_fusion.3), channel_id=1, source_target_pairs={{0,8},{8,0},{16,24},{24,16},{1,9},{9,1},{17,25},{25,17},{2,10},{10... | collective-permute-start | bytes 1720328 | tf_op jit(solution)/shard_map/ppermute | solution.py:29
  138.3 19.5 %collective-permute-start.9 = (bf16[80,1792]{1,0:T(8,128)(2,1)S(1)}, bf16[80,1792]{1,0:T(8,128)(2,1)S(1)}, u32[]{:S(2)}, u32[]{:S(2)}) collective-permute-start(bf16[80,1792]{1,0:T(8,128)(2,1)S(1)} %get-tuple-element.18), channel_id=1, source_target_pairs={{0,16},{8,24},{16,0},{24,8},{1,17},{9,25},{17,1},{25,9},{2,18},{10... | collective-permute-start | bytes 860168 | tf_op jit(solution)/shard_map/ppermute | solution.py:29
  138.4 27.4 %collective-permute-start.8 = (bf16[160,1792]{1,0:T(8,128)(2,1)S(1)}, bf16[160,1792]{1,0:T(8,128)(2,1)S(1)}, u32[]{:S(2)}, u32[]{:S(2)}) collective-permute-start(bf16[160,1792]{1,0:T(8,128)(2,1)S(1)} %pad_maximum_fusion.4), channel_id=1, source_target_pairs={{0,8},{8,0},{16,24},{24,16},{1,9},{9,1},{17,25},{25,17},{2,10},{10... | collective-permute-start | bytes 1720328 | tf_op jit(solution)/shard_map/ppermute | solution.py:29
  157.9 30.8 %collective-permute-start.11 = (bf16[160,1792]{1,0:T(8,128)(2,1)S(1)}, bf16[160,1792]{1,0:T(8,128)(2,1)}, u32[]{:S(2)}, u32[]{:S(2)}) collective-permute-start(bf16[160,1792]{1,0:T(8,128)(2,1)S(1)} %pad_maximum_fusion.5), channel_id=1, source_target_pairs={{0,8},{8,0},{16,24},{24,16},{1,9},{9,1},{17,25},{25,17},{2,10},{10... | collective-permute-start | bytes 1720328 | tf_op jit(solution)/shard_map/ppermute | solution.py:29
  177.6 12.3 %all-to-all-start.1 = ((bf16[8,32,1024]{2,1,0:T(8,128)(2,1)}), bf16[8,32,1024]{2,1,0:T(8,128)(2,1)S(1)}, u32[]{:S(2)}, u32[]{:S(2)}) async-start(bf16[8,32,1024]{2,1,0:T(8,128)(2,1)} %bitcast.92), calls=%async_computation.1 | async-start | bytes 1048576 | tf_op jit(solution)/shard_map/all_to_all | solution.py:170
  190.6 10.9 %all-to-all-start.2 = ((bf16[4,8,1024]{2,1,0:T(8,128)(2,1)}), bf16[4,8,1024]{2,1,0:T(8,128)(2,1)S(1)}, u32[]{:S(2)}, u32[]{:S(2)}) async-start(bf16[4,8,1024]{2,1,0:T(8,128)(2,1)} %bitcast.25), calls=%async_computation.2 | async-start | bytes 131072 | tf_op jit(solution)/shard_map/all_to_all | solution.py:178
